TPU v7x, 32 devices: a whole 2x2x4 slice. The times are simulated.
32 devices in a mesh: dp: 4 (over x, y), tp: 8 (over z, core).
Axes of the slice: x: 2, y: 2, z: 4, core: 2. Of those that a mesh axis runs over, the one named last changes fastest.
Arguments:
- x: bfloat16 [512, 8192], P('dp'), parts along dimension 0
- w_gate: bfloat16 [8192, 32768], P(None, 'tp')
- w_up: bfloat16 [8192, 32768], P(None, 'tp')
- w_down: bfloat16 [32768, 8192], P('tp')
Outputs:
- output: bfloat16 [512, 8192], P('dp'), parts along dimension 0
There are 4 independent parts. A program takes and returns all parts, laid end to end along the dimension named above; an argument that names none is the same for every part.
All inputs are finite; a program needn't handle non-finite values.
Results may differ from a plain program's by a relative error of at most 0.016.
Values are sent between devices in bfloat16 or wider.
A program may use at most 2 GiB of HBM per device.

v0:
```python
import jax
import jax.numpy as jnp
from jax import lax
from jax.sharding import PartitionSpec as P


def solution(mesh):
    def step(x, w_gate, w_up, w_down):
        gate = jnp.dot(x, w_gate, preferred_element_type=jnp.float32)
        up = jnp.dot(x, w_up, preferred_element_type=jnp.float32)
        hidden = (jax.nn.silu(gate) * up).astype(jnp.bfloat16)
        term = jnp.dot(hidden, w_down, preferred_element_type=jnp.float32).astype(jnp.bfloat16)
        return lax.psum(term, "tp")

    return jax.shard_map(
        step,
        mesh=mesh,
        in_specs=(P("dp", None), P(None, "tp"), P(None, "tp"), P("tp", None)),
        out_specs=P("dp", None),
        check_vma=False,
    )
```

profile of v0, /device:TPU:0, one launch (start us, length us, event | category | flops | bytes accessed | tf_op | source)
XLA Modules:
  0.0 158.1 jit_solution(8970387030978885536)
XLA Ops:
  6.5 0.0 copy-start
  6.5 0.0 all-reduce.2.cloned.1.call-start
  6.5 1.6 %copy-done = bf16[128,8192]{1,0:T(8,128)(2,1)S(1)} copy-done((bf16[128,8192]{1,0:T(8,128)(2,1)S(1)}, bf16[128,8192]{1,0:T(8,128)(2,1)}, u32[]{:S(2)}) %copy-start) | copy-done | bytes 2097176
  8.1 24.0 %fusion.8 = f32[128,4096]{1,0:T(8,128)} fusion(bf16[128,8192]{1,0:T(8,128)(2,1)S(1)} %copy-done, bf16[8192,4096]{1,0:T(8,128)(2,1)} %param.5), kind=kOutput, calls=%fused_computation.10 | convolution fusion | flops 8589934592 | bytes 71303168 | tf_op jit(solution)/shard_map/dot_general | solution.py:9
  32.2 23.9 %fusion.clone.4 = bf16[128,4096]{1,0:T(8,128)(2,1)S(1)} fusion(bf16[128,8192]{1,0:T(8,128)(2,1)S(1)} %copy-done, bf16[8192,4096]{1,0:T(8,128)(2,1)} %param.6, f32[128,4096]{1,0:T(8,128)} %fusion.8), kind=kOutput, calls=%fused_computation.2.clone.clone.clone.1 | convolution fusion | flops 8593080320 | bytes 72351744 | tf_op jit(solution)/shard_map/dot_general | solution.py:10
  56.0 24.3 %convolution_convert_fusion = bf16[128,8192]{1,0:T(8,128)(2,1)} fusion(bf16[4096,8192]{1,0:T(8,128)(2,1)} %param.7, bf16[128,4096]{1,0:T(8,128)(2,1)S(1)} %fusion.clone.4), kind=kOutput, calls=%fused_computation | convolution fusion | flops 8590983168 | bytes 70254592 | tf_op jit(solution)/shard_map/dot_general | solution.py:12
  80.3 0.0 all-reduce.2.cloned.1.call-update
  80.4 67.8 %all-reduce.2.cloned.1.call-done = bf16[128,8192]{1,0:T(8,128)(2,1)} async-done(((bf16[128,8192]{1,0:T(8,128)(2,1)}), bf16[128,8192]{1,0:T(8,128)(2,1)}) %all-reduce.2.cloned.1.call-update) | async-done | bytes 2097168 | tf_op jit(solution)/shard_map/psum | solution.py:13
  148.2 3.1 %copy.6 = bf16[128,8192]{1,0:T(8,128)(2,1)} copy(bf16[128,8192]{1,0:T(8,128)(2,1)} %all-reduce.2.cloned.1.call-done) | data formatting | bytes 4194304
Async XLA Ops:
  6.5 1.6 %copy-start = (bf16[128,8192]{1,0:T(8,128)(2,1)S(1)}, bf16[128,8192]{1,0:T(8,128)(2,1)}, u32[]{:S(2)}) copy-start(bf16[128,8192]{1,0:T(8,128)(2,1)} %param.4) | copy-start | bytes 6291460
  6.5 141.6 %all-reduce.2.cloned.1.call-start = ((), (), s32[]{:S(2)}) async-start(), calls=%async_computation | async-start | bytes 4194304 | tf_op jit(solution)/shard_map/psum | solution.py:13
Sparse Core Ops, SparseCore 0:
  80.5 67.6 all-reduce.1
where the time goes:
time: 158 us
  matrix products  72.2 us (46%)
  waiting for transfers between devices  67.8 us (43%)
  between operations  13.4 us (8%)
  local copies, waits for them, and re-layouts  4.68 us (3%)
    psum x1, waiting for transfers between devices, step(): return lax.psum(term, 'tp')  67.8 us
    dot_general x1, matrix products, step(): jnp.dot(hidden, w_down, preferred_element_type=jnp.float32)  24.3 us
    dot_general x1, matrix products, step(): gate = jnp.dot(x, w_gate, preferred_element_type=jnp.float32)  24 us
    dot_general x1, matrix products, step(): up = jnp.dot(x, w_up, preferred_element_type=jnp.float32)  23.9 us
    unnamed x3, local copies, waits for them, and re-layouts  4.68 us
  transfers between devices with their start and end apart: 1, of which 1 were waited for; matrix products, arithmetic and copies ran while one was open for 0% of the time, Pallas kernels for 0%

commit v1 on v0

v1 whole, which is shorter than its diff:
```python
import functools

import jax
import jax.numpy as jnp
from jax import lax
from jax.experimental import pallas as pl
from jax.experimental.pallas import tpu as pltpu
from jax.sharding import PartitionSpec as P

MESH = pl.DeviceIdType.MESH
BF16 = jnp.bfloat16
F32 = jnp.float32

KC = 512
NB = 5
NC = 512
ND = 6
PB = 4

PAIR, OUTER, INNER, MID, BACK, LAST = 2, 7, 11, 15, 19, 21


def kernel(
    x, wg, wu, wd, out,
    xb, gbuf, ubuf, dbuf, accg, accu, hid, pbuf, qbuf,
    send_p, recv_p, send_q, recv_q, send_z, recv_o, recv_m, fin, finp,
    sem_x, sem_g, sem_u, sem_d, sem_out, sem_outp,
    ss_x, rs_x, ss_y, rs_y, ss_f, rs_f,
    ss_p, rs_p, ss_qx, rs_qx, ss_qy, rs_qy,
    ss_z, rs_o, rs_m, ss_b, ss_fp, rs_fp,
):
    rows, d = x.shape
    half = rows // 2
    ff = wg.shape[1] // 2
    nk, nn = d // KC, d // NC
    hk, hn = KC // 2, NC // 2

    dp, tp = lax.axis_index("dp"), lax.axis_index("tp")
    z, core = tp // 2, tp % 2
    xn, yn = (dp + 2) % 4, dp + 1 - 2 * (dp % 2)
    mine = ((dp // 2 + dp) % 2) * ff
    pair = z * 2 + 1 - core
    near = (z + 1 - 2 * (z % 2)) * 2 + core
    across = (3 - z) * 2 + core
    inner = jnp.logical_or(z == 1, z == 2)
    outer = jnp.logical_not(inner)

    def gate_copy(k):
        slot = k % NB
        at = (pl.ds(pl.multiple_of(k * KC, KC), KC), pl.ds(pl.multiple_of(mine, ff), ff))
        return (
            pltpu.make_async_copy(wg.at[at], gbuf.at[slot], sem_g.at[slot]),
            pltpu.make_async_copy(wu.at[at], ubuf.at[slot], sem_u.at[slot]),
        )

    def down_copy(n):
        slot = n % ND
        at = (pl.ds(pl.multiple_of(mine, ff), ff), pl.ds(pl.multiple_of(n * NC, NC), NC))
        return pltpu.make_async_copy(wd.at[at], dbuf.at[slot], sem_d.at[slot])

    def remote(src, dst, ss, rs, **device):
        return pltpu.make_async_remote_copy(
            src_ref=src, dst_ref=dst, send_sem=ss, recv_sem=rs, device_id=device, device_id_type=MESH
        )

    def cols(k, c, width):
        return pl.ds(pl.multiple_of(k * 2 * width + c * width, width), width)

    def token_copies(k):
        at = cols(k, core, hk)
        return (
            remote(xb.at[pl.ds(0, half), at], xb.at[pl.ds(rows, half), at], ss_x.at[k], rs_x.at[k], dp=xn),
            remote(xb.at[pl.ds(half, half), at], xb.at[pl.ds(rows + half, half), at], ss_y.at[k], rs_y.at[k], dp=yn),
        )

    def pass_on(k):
        at = (pl.ds(rows, rows), cols(k, core, hk))
        return remote(xb.at[at], xb.at[at], ss_f.at[k], rs_f.at[k], tp=pair)

    def pair_copy(i):
        return remote(send_p.at[i], recv_p.at[i], ss_p.at[i], rs_p.at[i], tp=pair)

    def home_copies(i):
        return (
            remote(send_q.at[i, pl.ds(0, half)], recv_q.at[i, pl.ds(0, half)], ss_qx.at[i], rs_qx.at[i], dp=xn),
            remote(send_q.at[i, pl.ds(half, half)], recv_q.at[i, pl.ds(half, half)], ss_qy.at[i], rs_qy.at[i], dp=yn),
        )

    def in_copy(i):
        return remote(send_z.at[i], recv_o.at[i], ss_z.at[i], rs_o.at[i], tp=near)

    def mid_copy(i):
        return remote(send_z.at[i], recv_m.at[i], ss_z.at[i], rs_m.at[i], tp=across)

    def back_copy(i):
        return remote(fin.at[i], fin.at[i], ss_b.at[i], rs_o.at[i], tp=near)

    def share_copy(i):
        return remote(fin.at[i], finp.at[i], ss_fp.at[i], rs_fp.at[i], tp=pair)

    def out_copy(i):
        return pltpu.make_async_copy(fin.at[i], out.at[:, cols(i, core, hn)], sem_out.at[i])

    def outp_copy(i):
        return pltpu.make_async_copy(finp.at[i], out.at[:, cols(i, 1 - core, hn)], sem_outp.at[i])

    def loop(n, body):
        lax.fori_loop(0, n, lambda i, c: (body(i), c)[1], 0)

    own = pltpu.make_async_copy(x, xb.at[pl.ds(0, rows)], sem_x)
    own.start()
    for k in range(NB):
        for copy in gate_copy(k):
            copy.start()

    barrier = pltpu.get_barrier_semaphore()
    for device in ({"dp": xn}, {"dp": yn}, {"tp": pair}, {"tp": near}):
        pl.semaphore_signal(barrier, inc=1, device_id=device, device_id_type=MESH)

    @pl.when(inner)
    def _():
        pl.semaphore_signal(barrier, inc=1, device_id={"tp": across}, device_id_type=MESH)

    own.wait()

    @pl.when(outer)
    def _():
        pl.semaphore_wait(barrier, 4)

    @pl.when(inner)
    def _():
        pl.semaphore_wait(barrier, 5)

    @functools.partial(loop, nk)
    def _(k):
        for copy in token_copies(k):
            copy.start()

    accg[...] = jnp.zeros_like(accg)
    accu[...] = jnp.zeros_like(accu)

    def arrive(k):
        for copy in token_copies(k):
            copy.wait_recv()
        pass_on(k).start()

    arrive(0)

    def tokens(k):
        return xb[:, pl.ds(pl.multiple_of(k * KC, KC), KC)]

    @functools.partial(loop, nk - 1)
    def _(k):
        arrive(k + 1)
        pass_on(k).wait_recv()
        for copy in gate_copy(k):
            copy.wait()
        slot = k % NB
        accg[...] += jnp.dot(tokens(k), gbuf[slot], preferred_element_type=F32)
        accu[...] += jnp.dot(tokens(k), ubuf[slot], preferred_element_type=F32)

        @pl.when(k + NB < nk)
        def _():
            for copy in gate_copy(k + NB):
                copy.start()

        for j in range(2):
            n = (k - (nk - NB)) * 2 + j

            @pl.when(jnp.logical_and(n >= 0, n < ND))
            def _():
                down_copy(n).start()

    pass_on(nk - 1).wait_recv()
    for copy in gate_copy(nk - 1):
        copy.wait()
    slot = (nk - 1) % NB
    for j in range(ff // 512):
        at = pl.ds(j * 512, 512)
        gate = accg[:, at] + jnp.dot(tokens(nk - 1), gbuf[slot, :, at], preferred_element_type=F32)
        up = accu[:, at] + jnp.dot(tokens(nk - 1), ubuf[slot, :, at], preferred_element_type=F32)
        hid[:, at] = (jax.nn.silu(gate) * up).astype(BF16)

    def stage(j, lag, body, when=None):
        i = j - lag
        ok = jnp.logical_and(i >= 0, i < nn)
        pl.when(ok if when is None else jnp.logical_and(ok, when))(lambda: body(i))

    def down(i):
        down_copy(i).wait()
        p = jnp.dot(hid[...], dbuf[i % ND], preferred_element_type=F32)
        slot = i % PB
        pbuf[slot, 0] = p[:, :hn]
        pbuf[slot, 1] = p[:, hn:]
        send_p[i] = pbuf[slot, 1 - core].astype(BF16)
        pair_copy(i).start()

        @pl.when(i + ND < nn)
        def _():
            down_copy(i + ND).start()

    def pair_sum(i):
        pair_copy(i).wait_recv()
        slot = i % PB
        send_q[i] = (pbuf[slot, core, rows:, :] + recv_p[i, rows:, :].astype(F32)).astype(BF16)
        for copy in home_copies(i):
            copy.start()
        qbuf[i] = pbuf[slot, core, :rows, :] + recv_p[i, :rows, :].astype(F32)

    def home_sum(i):
        for copy in home_copies(i):
            copy.wait_recv()
        return qbuf[i] + recv_q[i].astype(F32)

    def outer_send(i):
        send_z[i] = home_sum(i).astype(BF16)
        in_copy(i).start()

    def inner_send(i):
        total = home_sum(i)
        in_copy(i).wait_recv()
        send_z[i] = (total + recv_o[i].astype(F32)).astype(BF16)
        mid_copy(i).start()

    def finish(i):
        share_copy(i).start()
        out_copy(i).start()

    def inner_finish(i):
        mid_copy(i).wait_recv()
        fin[i] = (send_z[i].astype(F32) + recv_m[i].astype(F32)).astype(BF16)
        back_copy(i).start()
        finish(i)

    def outer_finish(i):
        back_copy(i).wait_recv()
        finish(i)

    def last(i):
        share_copy(i).wait_recv()
        outp_copy(i).start()

    @functools.partial(loop, nn + LAST)
    def _(j):
        stage(j, 0, down)
        stage(j, PAIR, pair_sum)
        stage(j, OUTER, outer_send, outer)
        stage(j, INNER, inner_send, inner)
        stage(j, MID, inner_finish, inner)
        stage(j, BACK, outer_finish, outer)
        stage(j, LAST, last)

    @functools.partial(loop, nk)
    def _(k):
        for copy in token_copies(k):
            copy.wait_send()
        pass_on(k).wait_send()

    @functools.partial(loop, nn)
    def _(i):
        pair_copy(i).wait_send()
        for copy in home_copies(i):
            copy.wait_send()
        share_copy(i).wait_send()
        out_copy(i).wait()
        outp_copy(i).wait()

        @pl.when(inner)
        def _():
            mid_copy(i).wait_send()
            back_copy(i).wait_send()

        @pl.when(outer)
        def _():
            in_copy(i).wait_send()


def solution(mesh):
    def step(x, w_gate, w_up, w_down):
        rows, d = x.shape
        ff = w_gate.shape[1] // 2
        nk, nn, hn = d // KC, d // NC, NC // 2
        dma = pltpu.SemaphoreType.DMA
        any_space = pl.BlockSpec(memory_space=pl.ANY)
        flops = 2 * 3 * 2 * rows * d * ff
        return pl.pallas_call(
            kernel,
            name="mlp_sum",
            out_shape=jax.ShapeDtypeStruct((rows, d), BF16),
            in_specs=[any_space] * 4,
            out_specs=any_space,
            scratch_shapes=[
                pltpu.VMEM((2 * rows, d), BF16),
                pltpu.VMEM((NB, KC, ff), BF16),
                pltpu.VMEM((NB, KC, ff), BF16),
                pltpu.VMEM((ND, ff, NC), BF16),
                pltpu.VMEM((2 * rows, ff), F32),
                pltpu.VMEM((2 * rows, ff), F32),
                pltpu.VMEM((2 * rows, ff), BF16),
                pltpu.VMEM((PB, 2, 2 * rows, hn), F32),
                pltpu.VMEM((nn, rows, hn), F32),
                pltpu.VMEM((nn, 2 * rows, hn), BF16),
                pltpu.VMEM((nn, 2 * rows, hn), BF16),
                pltpu.VMEM((nn, rows, hn), BF16),
                pltpu.VMEM((nn, rows, hn), BF16),
                pltpu.VMEM((nn, rows, hn), BF16),
                pltpu.VMEM((nn, rows, hn), BF16),
                pltpu.VMEM((nn, rows, hn), BF16),
                pltpu.VMEM((nn, rows, hn), BF16),
                pltpu.VMEM((nn, rows, hn), BF16),
                dma, dma((NB,)), dma((NB,)), dma((ND,)), dma((nn,)), dma((nn,)),
                *[dma((nk,))] * 6,
                *[dma((nn,))] * 12,
            ],
            compiler_params=pltpu.CompilerParams(
                collective_id=0, has_side_effects=True, vmem_limit_bytes=64 * 1024 * 1024 - 65536
            ),
            cost_estimate=pl.CostEstimate(flops=flops, bytes_accessed=3 * d * ff * 2, transcendentals=0),
        )(x, w_gate, w_up, w_down)

    return jax.shard_map(
        step,
        mesh=mesh,
        in_specs=(P("dp", None), P(None, "tp"), P(None, "tp"), P("tp", None)),
        out_specs=P("dp", None),
        check_vma=False,
    )
```

time: 158 us -> 81 us (0.51)
  Pallas kernels: 0 us -> 77.3 us
  matrix products: 72.2 us -> 0 us
  waiting for transfers between devices: 67.8 us -> 0 us
  between operations: 13.4 us -> 0.01 us
    pallas_call x0 -> x1, Pallas kernels: none -> 77.3 us  [step(): pl.pallas_call(kernel, name='mlp_sum', out_shape=jax.ShapeDtypeStruct((ro...]
    dot_general x3 -> x0, matrix products: 72.2 us -> none  [the longest x1 24.3 us: step(): jnp.dot(hidden, w_down, preferred_element_type=jnp.float32)]
    psum x1 -> x0, waiting for transfers between devices: 67.8 us -> none  [step(): return lax.psum(term, 'tp')]
    unnamed x3 -> x1, local copies, waits for them, and re-layouts: 4.68 us -> 3.1 us
  transfers between devices with their start and end apart: 1 -> 0, of which waited for: 1 -> 0; matrix products, arithmetic and copies ran while one was open for 0% -> 0% of each run, Pallas kernels for 0% -> 0%
where the time goes in v1:
time: 81 us; the launch traced here: 80.5 us
  Pallas kernels  77.3 us (95%)
  local copies, waits for them, and re-layouts  3.1 us (4%)
    pallas_call x1, Pallas kernels, step(): pl.pallas_call(kernel, name='mlp_sum', out_shape=jax.ShapeDtypeStruct((ro...  77.3 us
    unnamed x1, local copies, waits for them, and re-layouts  3.1 us

profile of v1, /device:TPU:0, one launch (start us, length us, event | category | flops | bytes accessed | tf_op | source)
XLA Modules:
  0.0 80.5 jit_solution(12556773427619814060)
XLA Ops:
  0.0 77.3 %mlp_sum.1 = bf16[128,8192]{1,0:T(8,128)(2,1)} custom-call(bf16[128,8192]{1,0:T(8,128)(2,1)} %x.1, bf16[8192,4096]{1,0:T(8,128)(2,1)} %wg.1, bf16[8192,4096]{1,0:T(8,128)(2,1)} %wu.1, bf16[4096,8192]{1,0:T(8,128)(2,1)} %wd.1), custom_call_target="tpu_custom_call" | custom-call | flops 25769803776 | bytes 100663296 | tf_op jit(solution)/shard_map/mlp_sum/pallas_call | solution.py:286
  77.4 3.1 %copy.6 = bf16[128,8192]{1,0:T(8,128)(2,1)} copy(bf16[128,8192]{1,0:T(8,128)(2,1)} %mlp_sum.1) | data formatting | bytes 4194304

commit v2 on v1

v2 whole, which is shorter than its diff:
```python
import functools

import jax
import jax.numpy as jnp
from jax import lax
from jax.experimental import pallas as pl
from jax.experimental.pallas import tpu as pltpu
from jax.sharding import PartitionSpec as P

MESH = pl.DeviceIdType.MESH
BF16 = jnp.bfloat16
F32 = jnp.float32

KC = 512
NB = 5
EARLY = 3
NC = 512
ND = 6
PB = 2

SUB = 2
PAIR, OUTER, INNER, MID, BACK, LAST = 2, 8, 14, 19, 26, 28


def kernel(
    x, wg, wu, wd, out,
    xb, gbuf, ubuf, dbuf, accg, accu, hid, pbuf, qbuf,
    send_p, recv_p, send_q, recv_q, send_z, recv_o, recv_m,
    sem_x, sem_g, sem_u, sem_d,
    ss_t, rs_t, ss_f, rs_f,
    ss_p, rs_p, ss_q, rs_q, ss_z, rs_o, rs_m, ss_b, ss_s, rs_s,
):
    rows, d = x.shape
    half = rows // 2
    ff = wg.shape[1] // 2
    nk, nn = d // KC, d // NC
    hk, hn = KC // 2, NC // (2 * SUB)
    ns = nn * SUB

    dp, tp = lax.axis_index("dp"), lax.axis_index("tp")
    z, core = tp // 2, tp % 2
    xn, yn = (dp + 2) % 4, dp + 1 - 2 * (dp % 2)
    mine = ((dp // 2 + dp) % 2) * ff
    pair = z * 2 + 1 - core
    near = (z + 1 - 2 * (z % 2)) * 2 + core
    across = (3 - z) * 2 + core
    inner = jnp.logical_or(z == 1, z == 2)
    outer = jnp.logical_not(inner)

    def gate_copy(k):
        slot = k % NB
        at = (pl.ds(pl.multiple_of(k * KC, KC), KC), pl.ds(pl.multiple_of(mine, ff), ff))
        return (
            pltpu.make_async_copy(wg.at[at], gbuf.at[slot], sem_g.at[slot]),
            pltpu.make_async_copy(wu.at[at], ubuf.at[slot], sem_u.at[slot]),
        )

    def down_copy(n):
        slot = n % ND
        at = (pl.ds(pl.multiple_of(mine, ff), ff), pl.ds(pl.multiple_of(n * NC, NC), NC))
        return pltpu.make_async_copy(wd.at[at], dbuf.at[slot], sem_d.at[slot])

    def remote(src, dst, ss, rs, **device):
        return pltpu.make_async_remote_copy(
            src_ref=src, dst_ref=dst, send_sem=ss, recv_sem=rs, device_id=device, device_id_type=MESH
        )

    def cols(k, c, width):
        return pl.ds(pl.multiple_of(k * 2 * width + c * width, width), width)

    part = pl.ds(pl.multiple_of(core * hk, hk), hk)

    def token_copies(k):
        return (
            remote(xb.at[k, pl.ds(0, half), part], xb.at[k, pl.ds(rows, half), part], ss_t, rs_t.at[k], dp=xn),
            remote(xb.at[k, pl.ds(half, half), part], xb.at[k, pl.ds(rows + half, half), part], ss_t, rs_t.at[k], dp=yn),
        )

    def pass_on(k):
        at = (k, pl.ds(rows, rows), part)
        return remote(xb.at[at], xb.at[at], ss_f, rs_f.at[k], tp=pair)

    def both(k):
        at = (k, pl.ds(rows, rows), part)
        return remote(xb.at[at], xb.at[at], ss_t, rs_t.at[k], dp=xn)

    def pair_copy(i):
        return remote(send_p.at[i], recv_p.at[i], ss_p, rs_p.at[i], tp=pair)

    def home_copies(i):
        x_half, y_half = (i, pl.ds(0, half)), (i, pl.ds(half, half))
        return (
            remote(send_q.at[x_half], recv_q.at[x_half], ss_q, rs_q.at[i], dp=xn),
            remote(send_q.at[y_half], recv_q.at[y_half], ss_q, rs_q.at[i], dp=yn),
        )

    def in_copy(i):
        return remote(send_z.at[i], recv_o.at[i], ss_z, rs_o.at[i], tp=near)

    def mid_copy(i):
        return remote(send_z.at[i], recv_m.at[i], ss_z, rs_m.at[i], tp=across)

    def back_copy(i):
        at = (slice(None), cols(i, core, hn))
        return remote(out.at[at], out.at[at], ss_b, rs_o.at[i], tp=near)

    def share_copy(i):
        at = (slice(None), cols(i, core, hn))
        return remote(out.at[at], out.at[at], ss_s, rs_s.at[i], tp=pair)

    def loop(n, body):
        lax.fori_loop(0, n, lambda i, c: (body(i), c)[1], 0)

    barrier = pltpu.get_barrier_semaphore()
    for device in ({"dp": xn}, {"dp": yn}, {"tp": pair}, {"tp": near}):
        pl.semaphore_signal(barrier, inc=1, device_id=device, device_id_type=MESH)

    @pl.when(inner)
    def _():
        pl.semaphore_signal(barrier, inc=1, device_id={"tp": across}, device_id_type=MESH)

    @functools.partial(loop, nk)
    def _(k):
        at = pl.ds(pl.multiple_of(k * KC, KC), KC)
        pltpu.make_async_copy(x.at[:, at], xb.at[k, pl.ds(0, rows)], sem_x).start()

    for k in range(NB):
        for copy in gate_copy(k):
            copy.start()

    accg[...] = jnp.zeros_like(accg)
    accu[...] = jnp.zeros_like(accu)

    own = xb.at[:, pl.ds(0, rows)]
    pltpu.make_async_copy(own, own, sem_x).wait()

    @pl.when(outer)
    def _():
        pl.semaphore_wait(barrier, 4)

    @pl.when(inner)
    def _():
        pl.semaphore_wait(barrier, 5)

    @functools.partial(loop, nk)
    def _(k):
        for copy in token_copies(k):
            copy.start()

    def arrive(k):
        both(k).wait_recv()
        pass_on(k).start()

    def weights(k):
        for copy in gate_copy(k):
            copy.wait()

    def gate_up(k, at):
        slot = k % NB
        accg[at] += jnp.dot(xb[k, at], gbuf[slot], preferred_element_type=F32)
        accu[at] += jnp.dot(xb[k, at], ubuf[slot], preferred_element_type=F32)

    def refill(k):
        @pl.when(k + NB < nk)
        def _():
            for copy in gate_copy(k + NB):
                copy.start()

        for j in range(2):
            n = (k - (nk - NB)) * 2 + j

            @pl.when(jnp.logical_and(n >= 0, n < ND))
            def _():
                down_copy(n).start()

    @functools.partial(loop, EARLY)
    def _(k):
        weights(k)
        gate_up(k, pl.ds(0, rows))
        pl.when(k >= 1)(lambda: arrive(k - 1))

    arrive(EARLY - 1)

    @functools.partial(loop, EARLY)
    def _(k):
        arrive(k + EARLY)
        pass_on(k).wait_recv()
        gate_up(k, pl.ds(rows, rows))
        refill(k)

    @functools.partial(loop, nk - 1 - EARLY)
    def _(j):
        k = j + EARLY
        pl.when(k + EARLY < nk)(lambda: arrive(k + EARLY))
        pass_on(k).wait_recv()
        weights(k)
        gate_up(k, pl.ds(0, 2 * rows))
        refill(k)

    pass_on(nk - 1).wait_recv()
    weights(nk - 1)
    slot = (nk - 1) % NB
    for j in range(ff // 512):
        at = pl.ds(j * 512, 512)
        gate = accg[:, at] + jnp.dot(xb[nk - 1], gbuf[slot, :, at], preferred_element_type=F32)
        up = accu[:, at] + jnp.dot(xb[nk - 1], ubuf[slot, :, at], preferred_element_type=F32)
        hid[:, at] = (jax.nn.silu(gate) * up).astype(BF16)

    def stage(j, lag, body, when=None, n=ns):
        i = j - lag
        ok = jnp.logical_and(i >= 0, i < n)
        pl.when(ok if when is None else jnp.logical_and(ok, when))(lambda: body(i))

    def down(i):
        down_copy(i).wait()
        p = jnp.dot(hid[...], dbuf[i % ND], preferred_element_type=F32)
        for u in range(SUB):
            for c in range(2):
                pbuf[i % PB, u, c] = p[:, (2 * u + c) * hn : (2 * u + c + 1) * hn]
            send_p[SUB * i + u] = pbuf[i % PB, u, 1 - core].astype(BF16)
            pair_copy(SUB * i + u).start()

        @pl.when(i + ND < nn)
        def _():
            down_copy(i + ND).start()

    def pair_sum(i):
        pair_copy(i).wait_recv()
        mine_p = pbuf.at[(i // SUB) % PB, i % SUB, core]
        send_q[i] = (mine_p[rows:, :] + recv_p[i, rows:, :].astype(F32)).astype(BF16)
        for copy in home_copies(i):
            copy.start()
        qbuf[i] = mine_p[:rows, :] + recv_p[i, :rows, :].astype(F32)

    def home_sum(i):
        remote(send_q.at[i], recv_q.at[i], ss_q, rs_q.at[i], dp=xn).wait_recv()
        return qbuf[i] + recv_q[i].astype(F32)

    def outer_send(i):
        send_z[i] = home_sum(i).astype(BF16)
        in_copy(i).start()

    def inner_send(i):
        total = home_sum(i)
        in_copy(i).wait_recv()
        send_z[i] = (total + recv_o[i].astype(F32)).astype(BF16)
        mid_copy(i).start()

    def inner_finish(i):
        mid_copy(i).wait_recv()
        out[:, cols(i, core, hn)] = (send_z[i].astype(F32) + recv_m[i].astype(F32)).astype(BF16)
        back_copy(i).start()
        share_copy(i).start()

    def outer_finish(i):
        back_copy(i).wait_recv()
        share_copy(i).start()

    def last(i):
        share_copy(i).wait_recv()

    @functools.partial(loop, nn + (LAST + SUB - 1) // SUB)
    def _(j):
        stage(j, 0, down, n=nn)
        for u in range(SUB):
            i = SUB * j + u
            stage(i, PAIR, pair_sum)
            stage(i, OUTER, outer_send, outer)
            stage(i, INNER, inner_send, inner)
            stage(i, MID, inner_finish, inner)
            stage(i, BACK, outer_finish, outer)
            stage(i, LAST, last)

    tokens = xb.at[:, pl.ds(rows, rows), pl.ds(0, hk)]

    def sent(ref, ss):
        remote(ref, ref, ss, rs_p.at[0], tp=pair).wait_send()

    sent(tokens, ss_t)
    sent(tokens, ss_f)
    sent(send_p, ss_p)
    sent(send_q, ss_q)
    sent(send_z, ss_z)
    sent(send_z, ss_s)

    @pl.when(inner)
    def _():
        sent(send_z, ss_b)


def solution(mesh):
    def step(x, w_gate, w_up, w_down):
        rows, d = x.shape
        ff = w_gate.shape[1] // 2
        nk, ns, hn = d // KC, d // NC * SUB, NC // (2 * SUB)
        dma = pltpu.SemaphoreType.DMA
        any_space = pl.BlockSpec(memory_space=pl.ANY)
        flops = 2 * 3 * 2 * rows * d * ff
        return pl.pallas_call(
            kernel,
            name="mlp_sum",
            out_shape=pltpu.VMEM((rows, d), BF16),
            in_specs=[any_space] * 4,
            out_specs=pl.BlockSpec(memory_space=pltpu.VMEM),
            scratch_shapes=[
                pltpu.VMEM((nk, 2 * rows, KC), BF16),
                pltpu.VMEM((NB, KC, ff), BF16),
                pltpu.VMEM((NB, KC, ff), BF16),
                pltpu.VMEM((ND, ff, NC), BF16),
                pltpu.VMEM((2 * rows, ff), F32),
                pltpu.VMEM((2 * rows, ff), F32),
                pltpu.VMEM((2 * rows, ff), BF16),
                pltpu.VMEM((PB, SUB, 2, 2 * rows, hn), F32),
                pltpu.VMEM((ns, rows, hn), F32),
                pltpu.VMEM((ns, 2 * rows, hn), BF16),
                pltpu.VMEM((ns, 2 * rows, hn), BF16),
                pltpu.VMEM((ns, rows, hn), BF16),
                pltpu.VMEM((ns, rows, hn), BF16),
                pltpu.VMEM((ns, rows, hn), BF16),
                pltpu.VMEM((ns, rows, hn), BF16),
                pltpu.VMEM((ns, rows, hn), BF16),
                dma, dma((NB,)), dma((NB,)), dma((ND,)),
                dma, dma((nk,)), dma, dma((nk,)),
                dma, dma((ns,)), dma, dma((ns,)), dma, dma((ns,)), dma((ns,)), dma, dma, dma((ns,)),
            ],
            compiler_params=pltpu.CompilerParams(
                collective_id=0, has_side_effects=True, vmem_limit_bytes=60 * 1024 * 1024
            ),
            cost_estimate=pl.CostEstimate(flops=flops, bytes_accessed=3 * d * ff * 2, transcendentals=0),
        )(x, w_gate, w_up, w_down)

    return jax.shard_map(
        step,
        mesh=mesh,
        in_specs=(P("dp", None), P(None, "tp"), P(None, "tp"), P("tp", None)),
        out_specs=P("dp", None),
        check_vma=False,
    )
```

time: 81 us -> 69.7 us (0.86)
  Pallas kernels: 77.3 us -> 68.3 us
  local copies, waits for them, and re-layouts: 3.1 us -> 1.32 us
    pallas_call x1, Pallas kernels: 77.3 us -> 68.3 us  [step(): pl.pallas_call(kernel, name='mlp_sum', out_shape=pltpu.VMEM((rows, d), BF...]
    unnamed x1, local copies, waits for them, and re-layouts: 3.1 us -> 1.32 us
where the time goes in v2:
time: 69.7 us; the launch traced here: 69.6 us
  Pallas kernels  68.3 us (98%)
  local copies, waits for them, and re-layouts  1.32 us (2%)
    pallas_call x1, Pallas kernels, step(): pl.pallas_call(kernel, name='mlp_sum', out_shape=pltpu.VMEM((rows, d), BF...  68.3 us

profile of v2, /device:TPU:0, one launch (start us, length us, event | category | flops | bytes accessed | tf_op | source)
XLA Modules:
  0.0 69.6 jit_solution(9011273507935537624)
XLA Ops:
  0.0 68.3 %mlp_sum.1 = bf16[128,8192]{1,0:T(8,128)(2,1)S(1)} custom-call(bf16[128,8192]{1,0:T(8,128)(2,1)} %x.1, bf16[8192,4096]{1,0:T(8,128)(2,1)} %wg.1, bf16[8192,4096]{1,0:T(8,128)(2,1)} %wu.1, bf16[4096,8192]{1,0:T(8,128)(2,1)} %wd.1), custom_call_target="tpu_custom_call" | custom-call | flops 25769803776 | bytes 100663296 | tf_op jit(solution)/shard_map/mlp_sum/pallas_call | solution.py:299
  68.3 1.3 %copy.6 = bf16[128,8192]{1,0:T(8,128)(2,1)} copy(bf16[128,8192]{1,0:T(8,128)(2,1)S(1)} %mlp_sum.1) | data formatting | bytes 4194304
